TPU v7x, 16 devices: a whole 2x2x2 slice. The times are simulated.
16 devices in a mesh: dp: 1, ep: 16 (over x, y, z, core).
Axes of the slice: x: 2, y: 2, z: 2, core: 2. Of those that a mesh axis runs over, the one named last changes fastest.
Arguments:
- x: bfloat16 [1, 16, 256, 4096], P('dp', 'ep')
- expert: int32 [1, 16, 256, 8], P('dp', 'ep')
- slot: int32 [1, 16, 256, 8], P('dp', 'ep')
- gate: float32 [1, 16, 256, 8], P('dp', 'ep')
- w_gate: bfloat16 [64, 4096, 1408], P('ep')
- w_up: bfloat16 [64, 4096, 1408], P('ep')
- w_down: bfloat16 [64, 1408, 4096], P('ep')
- s_gate: bfloat16 [4096, 1408], replicated
- s_up: bfloat16 [4096, 1408], replicated
- s_down: bfloat16 [1408, 4096], replicated
Outputs:
- y: bfloat16 [1, 16, 256, 4096], P('dp', 'ep')
All inputs are finite; a program needn't handle non-finite values.
Results may differ from a plain program's by a relative error of at most 0.009.
Values are sent between devices in bfloat16 or wider.
A program may use at most 2 GiB of HBM per device.

v0:
```python
import jax
import jax.numpy as jnp
from jax import lax
from jax.sharding import NamedSharding, PartitionSpec as P


def einsum(form, a, b):
    return jnp.einsum(form, a.astype(jnp.float32), b.astype(jnp.float32))


def for_all(x, s_gate, s_up, s_down):
    h = jax.nn.silu(einsum("...d,df->...f", x, s_gate)) * einsum("...d,df->...f", x, s_up)
    return einsum("...f,fd->...d", h.astype(jnp.bfloat16), s_down)


def solution(mesh):
    def placed(v, *spec):
        return lax.with_sharding_constraint(v, NamedSharding(mesh, P(*spec)))

    def step(x, expert, slot, gate, w_gate, w_up, w_down, s_gate, s_up, s_down):
        experts, (tokens, top) = w_gate.shape[0], expert.shape[2:]
        slots = 5 * tokens * top // (4 * experts)
        to_expert = jax.nn.one_hot(expert, experts, dtype=jnp.bfloat16)
        to_slot = jax.nn.one_hot(slot, slots, dtype=jnp.bfloat16)
        weighted = to_expert * gate[..., None].astype(jnp.bfloat16)
        dispatch = einsum("abtke,abtkc->abtec", to_expert, to_slot).astype(jnp.bfloat16)
        combine = einsum("abtke,abtkc->abtec", weighted, to_slot).astype(jnp.bfloat16)
        z = einsum("abtec,abtd->aebcd", dispatch, x).astype(jnp.bfloat16)
        z = placed(z, "dp", None, "ep", None, None)
        z = placed(z, "dp", "ep", None, None, None)
        h = jax.nn.silu(einsum("aebcd,edf->aebcf", z, w_gate))
        h = (h * einsum("aebcd,edf->aebcf", z, w_up)).astype(jnp.bfloat16)
        out = einsum("aebcf,efd->aebcd", h, w_down).astype(jnp.bfloat16)
        out = placed(out, "dp", "ep", None, None, None)
        out = placed(out, "dp", None, "ep", None, None)
        y = einsum("abtec,aebcd->abtd", combine, out)
        return (y + for_all(x, s_gate, s_up, s_down)).astype(jnp.bfloat16)

    return step
```

profile of v0, /device:TPU:0, one launch (start us, length us, event | category | flops | bytes accessed | tf_op | source)
XLA Modules:
  0.0 772.1 jit_solution(5020620947983083076)
XLA Ops:
  0.0 0.0 copy-start
  0.0 1.0 copy.10
  1.0 0.0 copy-start.1
  1.0 0.8 copy.12
  1.8 0.0 copy-done.1
  1.8 0.0 copy-start.3
  1.9 0.6 copy-done.3
  2.5 3.6 convolution_convert_fusion.1
  6.1 5.6 copy.13
  11.8 0.0 copy-done
  11.8 9.9 %convolution_convert_fusion = bf16[64,40,4096]{2,1,0:T(8,128)(2,1)} fusion(bf16[256,64,40]{0,2,1:T(8,128)(2,1)S(1)} %copy.13, bf16[1,1,256,4096]{3,2,1,0:T(8,128)(2,1)S(1)} %copy-done), kind=kOutput, calls=%fused_computation.18 | convolution fusion | flops 5379194880 | bytes 24379392 | tf_op jit(solution)/abtec,abtd->aebcd/dot_general | solution.py:8
  21.7 235.5 %all-to-all.4 = bf16[1,16,4,1,40,4096]{5,4,2,3,0,1:T(8,128)(2,1)} all-to-all(bf16[1,16,4,1,40,4096]{5,4,2,3,0,1:T(8,128)(2,1)} %bitcast.137), channel_id=1, replica_groups=mesh['dp'=1,'ep'=16] {'ep'}, dimensions={1} | all-to-all | bytes 41943040 | tf_op jit(solution)/sharding_constraint;jit(solution)/sharding_constraint | solution.py:18
  257.2 40.8 %fusion.4 = f32[4,16,40,1408]{3,2,1,0:T(8,128)} fusion(bf16[4,4096,1408]{2,1,0:T(8,128)(2,1)} %param.4, bf16[1,16,4,1,40,4096]{5,4,2,3,0,1:T(8,128)(2,1)} %all-to-all.4), kind=kOutput, calls=%fused_computation.4 | convolution fusion | flops 29527900160 | bytes 81526784 | tf_op jit(solution)/aebcd,edf->aebcf/dot_general | solution.py:8
  298.0 41.6 %fusion.10 = bf16[1,4,16,40,1408]{4,3,2,1,0:T(8,128)(2,1)} fusion(f32[4,16,40,1408]{3,2,1,0:T(8,128)} %fusion.4, bf16[4,4096,1408]{2,1,0:T(8,128)(2,1)} %param.5, bf16[1,16,4,1,40,4096]{5,4,2,3,0,1:T(8,128)(2,1)} %all-to-all.4), kind=kOutput, calls=%fused_computation.12 | convolution fusion | flops 29549527040 | bytes 88735744 | tf_op jit(solution)/aebcd,edf->aebcf/dot_general | solution.py:8
  339.6 41.0 %convert_bitcast_fusion = bf16[1,4,16,1,40,4096]{5,4,2,1,3,0:T(8,128)(2,1)} fusion(bf16[4,1408,4096]{2,1,0:T(8,128)(2,1)} %param.6, bf16[1,4,16,40,1408]{4,3,2,1,0:T(8,128)(2,1)} %fusion.10), kind=kOutput, calls=%fused_computation.8 | convolution fusion | flops 29538385920 | bytes 74317824 | tf_op jit(solution)/aebcf,efd->aebcd/dot_general | solution.py:8
  380.6 17.5 %copy.16 = bf16[1,4,16,1,40,4096]{5,4,1,3,0,2:T(8,128)(2,1)} copy(bf16[1,4,16,1,40,4096]{5,4,2,1,3,0:T(8,128)(2,1)} %convert_bitcast_fusion) | data formatting | bytes 41943040 | tf_op jit(solution)/sharding_constraint;jit(solution)/sharding_constraint | solution.py:18
  398.1 0.0 copy-start.5
  398.1 0.0 copy-start.2
  398.1 0.0 copy-start.4
  398.1 6.2 all-to-all-start.1
  404.2 0.0 copy-done.5
  404.3 0.1 copy.11
  404.4 0.0 copy-done.2
  404.4 0.0 copy-done.4
  404.4 4.3 convolution_convert_fusion.2
  408.7 5.6 copy.23
  414.3 7.3 convolution_bitcast_fusion.2
  421.7 16.7 %fusion.37 = f32[256,4096]{1,0:T(8,128)} fusion(bf16[1408,4096]{1,0:T(8,128)(2,1)} %param.9, bf16[4096,1408]{1,0:T(8,128)(2,1)} %param.8, bf16[1,1,256,4096]{3,2,1,0:T(8,128)(2,1)S(1)} %copy-done, f32[1,256,1408]{2,1,0:T(8,128)} %convolution_bitcast_fusion.2), kind=kOutput, calls=%fused_computation.39 | convolution fusion | flops 5907742720 | bytes 30801920 | tf_op jit(solution)/...f,fd->...d/dot_general | solution.py:8
  438.4 319.2 %all-to-all-done.1 = bf16[1,4,16,1,40,4096]{5,4,1,3,0,2:T(8,128)(2,1)} async-done(((bf16[1,4,16,1,40,4096]{5,4,1,3,0,2:T(8,128)(2,1)}), bf16[1,4,16,1,40,4096]{5,4,1,3,0,2:T(8,128)(2,1)}, u32[]{:S(2)}, u32[]{:S(2)}) %all-to-all-start.1) | async-done | bytes 20971552 | tf_op jit(solution)/sharding_constraint;jit(solution)/sharding_constraint | solution.py:18
  757.6 14.4 %fusion.23 = bf16[1,1,256,4096]{3,2,1,0:T(8,128)(2,1)} fusion(f32[256,4096]{1,0:T(8,128)} %fusion.37, bf16[256,64,40]{0,2,1:T(8,128)(2,1)S(1)} %copy.23, bf16[64,40,4096]{2,1,0:T(8,128)(2,1)} %bitcast.38), kind=kOutput, calls=%fused_computation.23 | convolution fusion | flops 5370806272 | bytes 28573696 | tf_op jit(solution)/abtec,aebcd->abtd/dot_general | solution.py:8
  (1 shorter events, 0.0 us)
Async XLA Ops:
  0.0 11.8 %copy-start = (bf16[1,1,256,4096]{3,2,1,0:T(8,128)(2,1)S(1)}, bf16[1,1,256,4096]{3,2,1,0:T(8,128)(2,1)}, u32[]{:S(2)}) copy-start(bf16[1,1,256,4096]{3,2,1,0:T(8,128)(2,1)} %param.3) | copy-start | bytes 6291460
  1.0 0.9 copy-start.1
  1.8 0.7 copy-start.3
  398.1 6.2 copy-start.5
  398.1 6.3 copy-start.2
  398.1 6.3 copy-start.4
  398.1 359.6 %all-to-all-start.1 = ((bf16[1,4,16,1,40,4096]{5,4,1,3,0,2:T(8,128)(2,1)}), bf16[1,4,16,1,40,4096]{5,4,1,3,0,2:T(8,128)(2,1)}, u32[]{:S(2)}, u32[]{:S(2)}) async-start(bf16[1,4,16,1,40,4096]{5,4,1,3,0,2:T(8,128)(2,1)} %copy.16), calls=%async_computation.1 | async-start | bytes 41943040 | tf_op jit(solution)/sharding_constraint;jit(solution)/sharding_constraint | solution.py:18
where the time goes:
time: 772 us
  waiting for transfers between devices  319 us (41%)
  blocking collectives  236 us (31%)
  matrix products  180 us (23%)
  local copies, waits for them, and re-layouts  31.3 us (4%)
    another operation x1, waiting for transfers between devices, placed(): return lax.with_sharding_constraint(v, NamedSharding(mesh, P(*spec)))  319 us
    another operation x1, blocking collectives, placed(): return lax.with_sharding_constraint(v, NamedSharding(mesh, P(*spec)))  236 us
    dot_general x9, matrix products, einsum(): return jnp.einsum(form, a.astype(jnp.float32), b.astype(jnp.float32))  180 us
    another operation x1, local copies, waits for them, and re-layouts, placed(): return lax.with_sharding_constraint(v, NamedSharding(mesh, P(*spec)))  17.5 us
  transfers between devices with their start and end apart: 1, of which 1 were waited for; matrix products, arithmetic and copies ran while one was open for 4% of the time, Pallas kernels for 0%

commit v1 on v0

v1 whole, which is shorter than its diff:
```python
import functools

import jax
import jax.numpy as jnp
from jax import lax
from jax.experimental import pallas as pl
from jax.experimental.pallas import tpu as pltpu
from jax.sharding import PartitionSpec as P

MESH = pl.DeviceIdType.MESH
DK = 512
PARTS = ((0, 96), (96, 80), (176, 80))
LIMIT = 67_000_000
F32, BF16 = jnp.float32, jnp.bfloat16


class Place:
    def __init__(self):
        self.me = lax.axis_index("ep")
        self.bits = [lax.rem(lax.div(self.me, m), 2) for m in (8, 4, 2)]
        self.core = lax.rem(self.me, 2)
        self.partner = self.me + 1 - 2 * self.core

    def across(self, d):
        ids = [self.me + m * (1 - 2 * b) for m, b in zip((8, 4, 2), self.bits)]
        return ids[0] * lax.div((1 - d) * (2 - d), 2) + ids[1] * (d * (2 - d)) + ids[2] * lax.div(d * (d - 1), 2)

    def chip(self, m):
        ms = (lax.div(m, 4), lax.rem(lax.div(m, 2), 2), lax.rem(m, 2))
        x, y, z = (b + s * (1 - 2 * b) for b, s in zip(self.bits, ms))
        return ((x * 2 + y) * 2 + z) * 2


def turn(o, i):
    return lax.rem(o + i, 3)


def chip_at(o, pos):
    m = 0
    for i in range(3):
        if pos >> i & 1:
            d = turn(o, i)
            m = m + 4 - 2 * d + lax.div(d * (d - 1), 2)
    return m


def cols(k, width=DK):
    return pl.ds(pl.multiple_of(k * width, width), width)


def gather_kernel(
    x, route, wg, wu, sg, su,
    h_out, hs_out, g_out, r0, r1, r2, q0, q1, q2,
    rt, xv, z, wbuf, acc, accs, sbuf, gbuf, hbuf,
    route_send, route_recv, fill, send, recv1, recv2, recv3, drecv, load, wsem, gsem, hsem,
):
    at = Place()
    me = at.me
    tokens, d_model = x.shape
    chunks = d_model // DK
    experts, slots = 4, 40
    ff = wg.shape[2]
    r, q = (r0, r1, r2), (q0, q1, q2)

    def remote(src, dst, s, v, dev):
        return pltpu.make_async_remote_copy(
            src_ref=src, dst_ref=dst, send_sem=s, recv_sem=v, device_id={"ep": dev}, device_id_type=MESH
        )

    def first(k, p):
        row, size = PARTS[p]
        return remote(x.at[pl.ds(row, size), cols(k)], r[p].at[k, 1], send.at[0, p], recv1.at[p, k], at.across(turn(k, p)))

    def second(k, p):
        return remote(
            r[p].at[k, pl.ds(0, 2)], r[p].at[k, pl.ds(2, 2)], send.at[1, p], recv2.at[p, k], at.across(turn(k, p + 1))
        )

    def third(k, p):
        return remote(
            r[p].at[k, pl.ds(0, 4)], r[p].at[k, pl.ds(4, 4)], send.at[2, p], recv3.at[p, k], at.across(turn(k, p + 2))
        )

    def beside(k, p, i):
        half = pl.ds(4 * i, 4)
        return remote(r[p].at[k, half], q[p].at[k, half], send.at[3 + i, p], drecv.at[i, p, k], at.partner)

    def filled(k, p):
        row, size = PARTS[p]
        return pltpu.make_async_copy(x.at[pl.ds(row, size), cols(k)], r[p].at[k, 0], fill.at[p, k])

    def weights(i):
        slot = lax.rem(i, 3)
        left, right = wbuf.at[slot, :, pl.ds(0, ff)], wbuf.at[slot, :, pl.ds(ff, ff)]

        @pl.when(i < chunks)
        def _():
            rows = cols(i)
            pltpu.make_async_copy(sg.at[rows], left, wsem.at[slot]).start()
            pltpu.make_async_copy(su.at[rows], right, wsem.at[slot]).start()

        @pl.when(jnp.logical_and(i >= chunks, i < 5 * chunks))
        def _():
            j = i - chunks
            e, rows = lax.rem(j, 4), cols(lax.div(j, 4))
            pltpu.make_async_copy(wg.at[e, rows], left, wsem.at[slot]).start()
            pltpu.make_async_copy(wu.at[e, rows], right, wsem.at[slot]).start()

    def weights_ready(i):
        slot = lax.rem(i, 3)
        pltpu.make_async_copy(wbuf.at[slot], wbuf.at[slot], wsem.at[slot]).wait()
        weights(i + 2)
        return slot

    def load_rows(k, src, core, i):
        slot = lax.rem(k, 2)
        for p, (row, size) in enumerate(PARTS):
            o = turn(k, p)
            for pos in range(8):
                dst = xv.at[slot, chip_at(o, pos), pl.ds(pl.multiple_of(core * tokens + row, 16), size)]
                pltpu.make_async_copy(src[p].at[k, pos], dst, load.at[slot, i]).start()

    def rows_ready(k, i):
        slot = lax.rem(k, 2)
        half = xv.at[slot, :, pl.ds(0, tokens)]
        pltpu.make_async_copy(half, half, load.at[slot, i]).wait()

    weights(0)
    weights(1)
    for j in range(1, 16):
        dev = lax.rem(me + j, 16)
        remote(route, rt.at[me], route_send, route_recv.at[me], dev).start()
    rt[me] = route[...]
    for k in range(chunks):
        for p in range(3):
            filled(k, p).start()

    def build(m):
        base = at.chip(m)
        slot_of = lax.broadcasted_iota(jnp.int32, (80, tokens), 0)
        other = slot_of >= slots
        slot_of = jnp.where(other, slot_of - slots, slot_of)

        @pl.when(m >= 1)
        def _():
            pltpu.make_async_copy(gbuf, g_out.at[m - 1], gsem).wait()

        def one(e, _):
            want = (slot_of + (me * experts + e) * slots).astype(F32)
            rows = pl.ds(pl.multiple_of(e * 80, 80), 80)
            for c in range(2):
                here = jnp.where(other == (c == 1), want, -2.0)
                table = rt[base + c]
                s = jnp.zeros((80, tokens), F32)
                g = jnp.zeros((80, tokens), F32)
                for j in range(8):
                    hit = here == table[j : j + 1]
                    s = jnp.where(hit, 1.0, s)
                    g = jnp.where(hit, table[8 + j : 9 + j], g)
                sbuf[m, rows, c * tokens : (c + 1) * tokens] = s.astype(BF16)
                gbuf[rows, c * tokens : (c + 1) * tokens] = g.astype(BF16)
            return 0

        lax.fori_loop(0, experts, one, 0)
        pltpu.make_async_copy(gbuf, g_out.at[m], gsem).start()

    def clear(e, _):
        acc[e] = jnp.zeros(acc.shape[1:], F32)
        return 0

    def shared(i):
        slot = weights_ready(i)

        def tile(j, _):
            c = cols(j, 256)
            accs[:, c] += jnp.dot(x[:, cols(i)], wbuf[slot, :, c], preferred_element_type=F32)
            return 0

        lax.fori_loop(0, 2 * ff // 256, tile, 0)

    def compute(k):
        slot = lax.rem(k, 2)

        def dispatch(m, _):
            d = jnp.dot(sbuf[m], xv[slot, m], preferred_element_type=F32).astype(BF16)
            rows = pl.ds(pl.multiple_of(m * 80, 80), 80)
            for e in range(experts):
                z[e, rows] = d[e * 80 : (e + 1) * 80]
            return 0

        lax.fori_loop(0, 8, dispatch, 0)

        def expert(e, _):
            wslot = weights_ready(chunks + 4 * k + e)

            def tile(j, _):
                c = cols(j, 256)
                acc[e, :, c] += jnp.dot(z[e], wbuf[wslot, :, c], preferred_element_type=F32)
                return 0

            return lax.fori_loop(0, 2 * ff // 256, tile, 0)

        lax.fori_loop(0, experts, expert, 0)

    def step(s, _):
        @pl.when(s < chunks)
        def _():
            for p in range(3):
                first(s, p).start()

        @pl.when(jnp.logical_and(s >= 1, s < chunks + 1))
        def _():
            k = s - 1
            for p in range(3):
                filled(k, p).wait()
                first(k, p).wait_recv()
                second(k, p).start()

        @pl.when(jnp.logical_and(s >= 2, s < chunks + 2))
        def _():
            k = s - 2
            for p in range(3):
                second(k, p).wait_recv()
                third(k, p).start()
                beside(k, p, 0).start()

        @pl.when(s == 0)
        def _():
            accs[...] = jnp.zeros(accs.shape, F32)

        @pl.when(s < 4)
        def _():
            clear(s, 0)
            shared(2 * s)
            shared(2 * s + 1)

        @pl.when(s == 2)
        def _():
            for j in range(1, 16):
                b = lax.rem(me + j, 16)
                remote(route, rt.at[b], route_send, route_recv.at[b], b).wait_recv()

            def one(m, _):
                build(m)
                return 0

            lax.fori_loop(0, 8, one, 0)
            pltpu.make_async_copy(gbuf, g_out.at[7], gsem).wait()

        @pl.when(jnp.logical_and(s >= 3, s < chunks + 3))
        def _():
            k = s - 3
            for p in range(3):
                third(k, p).wait_recv()
                beside(k, p, 1).start()
            load_rows(k, r, at.core, 0)

        @pl.when(s >= 4)
        def _():
            k = s - 4
            for p in range(3):
                beside(k, p, 0).wait_recv()
                beside(k, p, 1).wait_recv()
            load_rows(k, q, 1 - at.core, 1)
            rows_ready(k, 0)
            rows_ready(k, 1)
            compute(k)

        return 0

    lax.fori_loop(0, chunks + 4, step, 0)

    def hidden(src, dst, i, rows):
        slot = lax.rem(i, 2)

        @pl.when(i >= 2)
        def _():
            pltpu.make_async_copy(hbuf.at[slot], dst, hsem.at[slot]).wait()

        a = src[rows, pl.ds(0, ff)]
        hbuf[slot] = (a * jax.nn.sigmoid(a) * src[rows, pl.ds(ff, ff)]).astype(BF16)
        pltpu.make_async_copy(hbuf.at[slot], dst, hsem.at[slot]).start()

    def routed(i, _):
        e, rows = lax.div(i, 10), pl.ds(pl.multiple_of(lax.rem(i, 10) * 64, 64), 64)
        hidden(acc.at[e], h_out.at[e, rows], i, rows)
        return 0

    lax.fori_loop(0, 10 * experts, routed, 0)

    def common(i, _):
        rows = pl.ds(pl.multiple_of(i * 64, 64), 64)
        hidden(accs, hs_out.at[rows], i + 10 * experts, rows)
        return 0

    lax.fori_loop(0, tokens // 64, common, 0)
    for slot in range(2):
        pltpu.make_async_copy(hbuf.at[slot], hs_out.at[pl.ds(0, 64)], hsem.at[slot]).wait()

    remote(rt.at[pl.ds(0, 15)], rt.at[pl.ds(0, 15)], route_send, route_recv.at[0], at.partner).wait_send()
    for p in range(3):
        one, two, four, rest = r[p].at[:, 0], r[p].at[:, pl.ds(0, 2)], r[p].at[:, pl.ds(0, 4)], r[p].at[:, pl.ds(4, 4)]
        for i, sent in enumerate((one, two, four, four, rest)):
            remote(sent, sent, send.at[i, p], recv1.at[p, 0], at.partner).wait_send()


def scatter_kernel(
    h, hs, g, wd, sd,
    y,
    hv, hsv, gv, wbuf, o, dsend, dland, acc8, acc4, acc2, acc1,
    as0, as1, as2, bs0, bs1, bs2, cs0, cs1, cs2,
    al0, al1, al2, bl0, bl1, bl2, cl0, cl1, cl2,
    start_sem, wsem, dsend_sem, drecv, free, asend_sem, bsend_sem, csend_sem, arecv, brecv, crecv,
):
    at = Place()
    tokens, d_model = y.shape
    chunks = d_model // DK
    experts = h.shape[0]
    ff = h.shape[2]
    a_send, b_send, c_send = (as0, as1, as2), (bs0, bs1, bs2), (cs0, cs1, cs2)
    a_land, b_land, c_land = (al0, al1, al2), (bl0, bl1, bl2), (cl0, cl1, cl2)

    def remote(src, dst, s, v, dev):
        return pltpu.make_async_remote_copy(
            src_ref=src, dst_ref=dst, send_sem=s, recv_sem=v, device_id={"ep": dev}, device_id_type=MESH
        )

    def beside(k):
        slot = lax.rem(k, 2)
        return remote(dsend.at[slot], dland.at[slot], dsend_sem.at[slot], drecv.at[slot], at.partner)

    def hop(stage, k, p):
        slot = lax.rem(k, 2)
        src, dst = (a_send, b_send, c_send)[stage][p], (a_land, b_land, c_land)[stage][p]
        sems, lands = (asend_sem, bsend_sem, csend_sem)[stage], (arecv, brecv, crecv)[stage]
        return remote(src.at[slot], dst.at[k], sems.at[p, slot], lands.at[p, k], at.across(turn(k, p + 2 - stage)))

    def weights(i):
        slot = lax.rem(i, 3)
        k, e = lax.div(i, 5), lax.rem(i, 5)

        @pl.when(jnp.logical_and(i < 5 * chunks, e < 4))
        def _():
            pltpu.make_async_copy(wd.at[e, :, cols(k)], wbuf.at[slot], wsem.at[slot]).start()

        @pl.when(jnp.logical_and(i < 5 * chunks, e == 4))
        def _():
            pltpu.make_async_copy(sd.at[:, cols(k)], wbuf.at[slot], wsem.at[slot]).start()

    def weights_ready(i):
        slot = lax.rem(i, 3)
        pltpu.make_async_copy(wbuf.at[slot], wbuf.at[slot], wsem.at[slot]).wait()
        weights(i + 2)
        return slot

    begin = [
        pltpu.make_async_copy(h, hv, start_sem.at[0]),
        pltpu.make_async_copy(hs, hsv, start_sem.at[1]),
        pltpu.make_async_copy(g, gv, start_sem.at[2]),
    ]
    weights(0)
    for copy in begin:
        copy.start()
    weights(1)
    for copy in begin:
        copy.wait()

    def compute(k):
        slot = lax.rem(k, 2)

        def expert(e, _):
            wslot = weights_ready(5 * k + e)

            def tile(j, _):
                c = cols(j, 256)
                o[e, :, c] = jnp.dot(hv[e], wbuf[wslot, :, c], preferred_element_type=F32).astype(BF16)
                return 0

            return lax.fori_loop(0, DK // 256, tile, 0)

        lax.fori_loop(0, experts, expert, 0)

        @pl.when(k >= 2)
        def _():
            beside(k).wait_send()

        def combine(m, _):
            rows = o[:, pl.ds(pl.multiple_of(m * 80, 80), 80), :].reshape(4 * 80, DK)
            mine = gv[m, :, cols(at.core, 256)]
            theirs = gv[m, :, cols(1 - at.core, 256)]
            across = (((0,), (0,)), ((), ()))
            acc8[m] = lax.dot_general(mine, rows, across, preferred_element_type=F32)
            dsend[slot, m] = lax.dot_general(theirs, rows, across, preferred_element_type=F32).astype(BF16)
            return 0

        lax.fori_loop(0, 8, combine, 0)

        @pl.when(k >= 2)
        def _():
            pl.semaphore_wait(free, 1)

        beside(k).start()

        wslot = weights_ready(5 * k + 4)

        def tile(j, _):
            c = cols(j, 256)
            acc8[0, :, c] += jnp.dot(hsv[...], wbuf[wslot, :, c], preferred_element_type=F32)
            return 0

        lax.fori_loop(0, DK // 256, tile, 0)

    def send_when_free(stage, k, p):
        @pl.when(k >= 2)
        def _():
            hop(stage, k, p).wait_send()

    def first(k):
        slot = lax.rem(k, 2)
        beside(k).wait_recv()
        for p, (row, size) in enumerate(PARTS):
            send_when_free(0, k, p)
            for pos in range(7, -1, -1):
                m = chip_at(turn(k, p), pos)
                v = acc8[m, row : row + size] + dland[slot, m, row : row + size].astype(F32)
                if pos >= 4:
                    a_send[p][slot, pos - 4] = v.astype(BF16)
                else:
                    acc4[slot, pos, row : row + size] = v
                if pos == 4:
                    hop(0, k, p).start()

        @pl.when(k + 2 < chunks)
        def _():
            pl.semaphore_signal(free, inc=1, device_id={"ep": at.partner}, device_id_type=MESH)

    def second(k):
        slot = lax.rem(k, 2)
        for p, (row, size) in enumerate(PARTS):
            hop(0, k, p).wait_recv()
            send_when_free(1, k, p)
            for pos in range(3, -1, -1):
                v = acc4[slot, pos, row : row + size] + a_land[p][k, pos].astype(F32)
                if pos >= 2:
                    b_send[p][slot, pos - 2] = v.astype(BF16)
                else:
                    acc2[slot, pos, row : row + size] = v
                if pos == 2:
                    hop(1, k, p).start()

    def third(k):
        slot = lax.rem(k, 2)
        for p, (row, size) in enumerate(PARTS):
            hop(1, k, p).wait_recv()
            send_when_free(2, k, p)
            for pos in (1, 0):
                v = acc2[slot, pos, row : row + size] + b_land[p][k, pos].astype(F32)
                if pos == 1:
                    c_send[p][slot, 0] = v.astype(BF16)
                    hop(2, k, p).start()
                else:
                    acc1[slot, row : row + size] = v

    def last(k):
        slot = lax.rem(k, 2)
        for p, (row, size) in enumerate(PARTS):
            hop(2, k, p).wait_recv()
            y[row : row + size, cols(k)] = (acc1[slot, row : row + size] + c_land[p][k, 0].astype(F32)).astype(BF16)

    def step(s, _):
        for stage, work in ((1, first), (0, compute), (2, second), (3, third), (4, last)):

            @pl.when(jnp.logical_and(s >= stage, s < chunks + stage))
            def _():
                work(s - stage)

        return 0

    lax.fori_loop(0, chunks + 4, step, 0)
    for k in (chunks - 2, chunks - 1):
        beside(k).wait_send()
        for stage in range(3):
            for p in range(3):
                hop(stage, k, p).wait_send()


def layer(x, expert, slot, gate, w_gate, w_up, w_down, s_gate, s_up, s_down):
    tokens, d_model = x.shape[2:]
    top = expert.shape[3]
    experts, _, ff = w_gate.shape
    slots = 5 * tokens * top // (4 * 64)
    chunks = d_model // DK
    rows = 16 * slots
    x = x.reshape(tokens, d_model)
    kept = jnp.where(slot < slots, expert * slots + slot, -1).astype(F32)
    route = jnp.concatenate([kept.reshape(tokens, top), gate.reshape(tokens, top)], axis=1).T

    dma, vmem, anyw = pltpu.SemaphoreType.DMA, pltpu.VMEM, pl.BlockSpec(memory_space=pl.ANY)
    here = pl.BlockSpec(memory_space=pltpu.VMEM)
    shape = jax.ShapeDtypeStruct
    landing = [shape((chunks, 8, size, DK), BF16) for _, size in PARTS]
    h, hs, g, *_ = pl.pallas_call(
        gather_kernel,
        name="gather_up",
        out_shape=[shape((experts, rows, ff), BF16), shape((tokens, ff), BF16), shape((8, 8 * slots, 2 * tokens), BF16)]
        + landing * 2,
        in_specs=[here, here] + [anyw] * 4,
        out_specs=[anyw] * 9,
        scratch_shapes=[
            vmem((16, 2 * top, tokens), F32),
            vmem((2, 8, 2 * tokens, DK), BF16),
            vmem((experts, rows, DK), BF16),
            vmem((3, DK, 2 * ff), BF16),
            vmem((experts, rows, 2 * ff), F32),
            vmem((tokens, 2 * ff), F32),
            vmem((8, 8 * slots, 2 * tokens), BF16),
            vmem((8 * slots, 2 * tokens), BF16),
            vmem((2, 64, ff), BF16),
            dma,
            dma((16,)),
            dma((3, chunks)),
            dma((5, 3)),
            dma((3, chunks)),
            dma((3, chunks)),
            dma((3, chunks)),
            dma((2, 3, chunks)),
            dma((2, 2)),
            dma((3,)),
            dma,
            dma((2,)),
        ],
        compiler_params=pltpu.CompilerParams(has_side_effects=True, vmem_limit_bytes=LIMIT),
    )(x, route, w_gate, w_up, s_gate, s_up)

    def by_part(lead, count):
        return [vmem((lead, count, size, DK), BF16) for _, size in PARTS]

    y = pl.pallas_call(
        scatter_kernel,
        name="down_scatter",
        out_shape=shape((tokens, d_model), BF16),
        in_specs=[anyw] * 5,
        out_specs=here,
        scratch_shapes=[
            vmem((experts, rows, ff), BF16),
            vmem((tokens, ff), BF16),
            vmem((8, 8 * slots, 2 * tokens), BF16),
            vmem((3, ff, DK), BF16),
            vmem((experts, rows, DK), BF16),
            vmem((2, 8, tokens, DK), BF16),
            vmem((2, 8, tokens, DK), BF16),
            vmem((8, tokens, DK), F32),
            vmem((2, 4, tokens, DK), F32),
            vmem((2, 2, tokens, DK), F32),
            vmem((2, tokens, DK), F32),
            *by_part(2, 4), *by_part(2, 2), *by_part(2, 1),
            *by_part(chunks, 4), *by_part(chunks, 2), *by_part(chunks, 1),
            dma((3,)),
            dma((3,)),
            dma((2,)),
            dma((2,)),
            pltpu.SemaphoreType.REGULAR,
            dma((3, 2)),
            dma((3, 2)),
            dma((3, 2)),
            dma((3, chunks)),
            dma((3, chunks)),
            dma((3, chunks)),
        ],
        compiler_params=pltpu.CompilerParams(has_side_effects=True, vmem_limit_bytes=LIMIT),
    )(h, hs, g, w_down, s_down)
    return y.reshape(1, 1, tokens, d_model)


def solution(mesh):
    by_device, by_expert = P("dp", "ep", None, None), P("ep", None, None)
    return jax.shard_map(
        layer,
        mesh=mesh,
        in_specs=(by_device,) * 4 + (by_expert,) * 3 + (P(None, None),) * 3,
        out_specs=by_device,
        check_vma=False,
    )
```

time: 772 us -> 383 us (0.50)
  Pallas kernels: 0 us -> 377 us
  waiting for transfers between devices: 319 us -> 0 us
  blocking collectives: 236 us -> 0 us
  matrix products: 180 us -> 0 us
  local copies, waits for them, and re-layouts: 31.3 us -> 3.13 us
    pallas_call x0 -> x2, Pallas kernels: none -> 377 us  [the longest x1 233 us: layer(): pl.pallas_call(gather_kernel, name='gather_up', out_shape=[shape((experts...]
    another operation x1 -> x0, waiting for transfers between devices: 319 us -> none  [placed(): return lax.with_sharding_constraint(v, NamedSharding(mesh, P(*spec)))]
    another operation x1 -> x0, blocking collectives: 236 us -> none  [placed(): return lax.with_sharding_constraint(v, NamedSharding(mesh, P(*spec)))]
    dot_general x9 -> x0, matrix products: 180 us -> none  [einsum(): return jnp.einsum(form, a.astype(jnp.float32), b.astype(jnp.float32))]
    another operation x1 -> x0, local copies, waits for them, and re-layouts: 17.5 us -> none  [placed(): return lax.with_sharding_constraint(v, NamedSharding(mesh, P(*spec)))]
    convert_element_type x3 -> x0, local copies, waits for them, and re-layouts: 11.4 us -> none  [the longest x1 5.62 us: step(): einsum('abtke,abtkc->abtec', to_expert, to_slot).astype(jnp.bfloat16)]
  transfers between devices with their start and end apart: 1 -> 0, of which waited for: 1 -> 0; matrix products, arithmetic and copies ran while one was open for 4% -> 0% of each run, Pallas kernels for 0% -> 0%
where the time goes in v1:
time: 383 us; the launch traced here: 382 us
  Pallas kernels  377 us (98%)
    pallas_call x1, Pallas kernels, layer(): pl.pallas_call(gather_kernel, name='gather_up', out_shape=[shape((experts...  233 us
    pallas_call x1, Pallas kernels, layer(): pl.pallas_call(scatter_kernel, name='down_scatter', out_shape=shape((toke...  144 us

profile of v1, /device:TPU:0, one launch (start us, length us, event | category | flops | bytes accessed | tf_op | source)
XLA Modules:
  0.0 382.3 jit_solution(6129392553016728177)
XLA Ops:
  0.0 0.7 convert_bitcast_fusion
  0.7 1.3 maximum_bitcast_fusion.route
  2.0 233.5 %gather_up.1 = (bf16[4,640,1408]{2,1,0:T(8,128)(2,1)}, bf16[256,1408]{1,0:T(8,128)(2,1)}, bf16[8,320,512]{2,1,0:T(8,128)(2,1)}, bf16[8,8,96,512]{3,2,1,0:T(8,128...) custom-call(bf16[256,4096]{1,0:T(8,128)(2,1)} %bitcast.8, ...), custom_call_target="tpu_custom_call" | custom-call | tf_op jit(solution)/shard_map/gather_up/pallas_call | solution.py:502
  235.5 143.7 %down_scatter.1 = bf16[256,4096]{1,0:T(8,128)(2,1)} custom-call(bf16[4,640,1408]{2,1,0:T(8,128)(2,1)} %get-tuple-element.8.h, bf16[256,1408]{1,0:T(8,128)(2,1)} %get-tuple-element.9.hs, bf16[8,320,512]{2,1,0:T(8,128)(2,1)} %get-tuple-element.10.g, bf16[4,1408,4096]{2,1,0:T(8,128)(2,1)} %wd.1, bf16[1408,4096]{1,0:T(8,128)(2,1)} %sd.1), custom_call_target="tpu_custom_call" | custom-call | tf_op jit(solution)/shard_map/down_scatter/pallas_call | solution.py:538
  379.2 3.1 copy.12

commit v2 on v1

--- a/solution.py
+++ b/solution.py
@@ -131,6 +131,8 @@
         dev = lax.rem(me + j, 16)
         remote(route, rt.at[me], route_send, route_recv.at[me], dev).start()
     rt[me] = route[...]
+    for p in range(3):
+        first(0, p).start()
     for k in range(chunks):
         for p in range(3):
             filled(k, p).start()
@@ -144,6 +146,15 @@
         @pl.when(m >= 1)
         def _():
             pltpu.make_async_copy(gbuf, g_out.at[m - 1], gsem).wait()
+
+        row = lax.broadcasted_iota(jnp.int32, (experts * slots, tokens), 0)
+        for c in range(2):
+            table = rt[base + c]
+            want = (row + me * (experts * slots)).astype(F32)
+            s = jnp.zeros((experts * slots, tokens), F32)
+            for j in range(8):
+                s = jnp.where(want == table[j : j + 1], 1.0, s)
+            sbuf[m, c] = s.astype(BF16)
 
         def one(e, _):
             want = (slot_of + (me * experts + e) * slots).astype(F32)
@@ -151,13 +162,9 @@
             for c in range(2):
                 here = jnp.where(other == (c == 1), want, -2.0)
                 table = rt[base + c]
-                s = jnp.zeros((80, tokens), F32)
                 g = jnp.zeros((80, tokens), F32)
                 for j in range(8):
-                    hit = here == table[j : j + 1]
-                    s = jnp.where(hit, 1.0, s)
-                    g = jnp.where(hit, table[8 + j : 9 + j], g)
-                sbuf[m, rows, c * tokens : (c + 1) * tokens] = s.astype(BF16)
+                    g = jnp.where(here == table[j : j + 1], table[8 + j : 9 + j], g)
                 gbuf[rows, c * tokens : (c + 1) * tokens] = g.astype(BF16)
             return 0
 
@@ -170,43 +177,51 @@
 
     def shared(i):
         slot = weights_ready(i)
-
-        def tile(j, _):
-            c = cols(j, 256)
-            accs[:, c] += jnp.dot(x[:, cols(i)], wbuf[slot, :, c], preferred_element_type=F32)
+        accs[...] += jnp.dot(x[:, cols(i)], wbuf[slot], preferred_element_type=F32)
+
+    def gathered(k):
+        @pl.when(k < chunks)
+        def _():
+            for p in range(3):
+                third(k, p).wait_recv()
+                beside(k, p, 1).start()
+            load_rows(k, r, at.core, 0)
+
+    def exchanged(k):
+        @pl.when(k < chunks)
+        def _():
+            for p in range(3):
+                beside(k, p, 0).wait_recv()
+                beside(k, p, 1).wait_recv()
+            load_rows(k, q, 1 - at.core, 1)
+
+    def compute(k):
+        slot = lax.rem(k, 2)
+
+        for m in range(8):
+            d = [
+                jnp.dot(sbuf[m, c], xv[slot, m, c * tokens : (c + 1) * tokens], preferred_element_type=F32)
+                for c in range(2)
+            ]
+            for e in range(experts):
+                mine = [v[e * slots : (e + 1) * slots] for v in d]
+                z[e, m * 80 : (m + 1) * 80] = jnp.concatenate(mine, axis=0).astype(BF16)
+
+        def expert(e, _):
+            pl.when(e == 1)(lambda: gathered(k + 1))
+            pl.when(e == 3)(lambda: exchanged(k + 1))
+            wslot = weights_ready(chunks + 4 * k + e)
+
+            acc[e] += jnp.dot(z[e], wbuf[wslot], preferred_element_type=F32)
             return 0
 
-        lax.fori_loop(0, 2 * ff // 256, tile, 0)
-
-    def compute(k):
-        slot = lax.rem(k, 2)
-
-        def dispatch(m, _):
-            d = jnp.dot(sbuf[m], xv[slot, m], preferred_element_type=F32).astype(BF16)
-            rows = pl.ds(pl.multiple_of(m * 80, 80), 80)
-            for e in range(experts):
-                z[e, rows] = d[e * 80 : (e + 1) * 80]
-            return 0
-
-        lax.fori_loop(0, 8, dispatch, 0)
-
-        def expert(e, _):
-            wslot = weights_ready(chunks + 4 * k + e)
-
-            def tile(j, _):
-                c = cols(j, 256)
-                acc[e, :, c] += jnp.dot(z[e], wbuf[wslot, :, c], preferred_element_type=F32)
-                return 0
-
-            return lax.fori_loop(0, 2 * ff // 256, tile, 0)
-
         lax.fori_loop(0, experts, expert, 0)
 
     def step(s, _):
-        @pl.when(s < chunks)
+        @pl.when(s + 1 < chunks)
         def _():
             for p in range(3):
-                first(s, p).start()
+                first(s + 1, p).start()
 
         @pl.when(jnp.logical_and(s >= 1, s < chunks + 1))
         def _():
@@ -247,21 +262,14 @@
             lax.fori_loop(0, 8, one, 0)
             pltpu.make_async_copy(gbuf, g_out.at[7], gsem).wait()
 
-        @pl.when(jnp.logical_and(s >= 3, s < chunks + 3))
-        def _():
-            k = s - 3
-            for p in range(3):
-                third(k, p).wait_recv()
-                beside(k, p, 1).start()
-            load_rows(k, r, at.core, 0)
+        @pl.when(s == 3)
+        def _():
+            gathered(0)
+            exchanged(0)
 
         @pl.when(s >= 4)
         def _():
             k = s - 4
-            for p in range(3):
-                beside(k, p, 0).wait_recv()
-                beside(k, p, 1).wait_recv()
-            load_rows(k, q, 1 - at.core, 1)
             rows_ready(k, 0)
             rows_ready(k, 1)
             compute(k)
@@ -353,62 +361,54 @@
         weights(i + 2)
         return slot
 
-    begin = [
-        pltpu.make_async_copy(h, hv, start_sem.at[0]),
-        pltpu.make_async_copy(hs, hsv, start_sem.at[1]),
-        pltpu.make_async_copy(g, gv, start_sem.at[2]),
-    ]
+    def hidden(e):
+        return pltpu.make_async_copy(h.at[e], hv.at[e], start_sem.at[e])
+
+    common = pltpu.make_async_copy(hs, hsv, start_sem.at[4])
+    gates = pltpu.make_async_copy(g, gv, start_sem.at[5])
+    hidden(0).start()
     weights(0)
-    for copy in begin:
+    hidden(1).start()
+    weights(1)
+    for copy in (hidden(2), hidden(3), gates, common):
         copy.start()
-    weights(1)
-    for copy in begin:
-        copy.wait()
 
     def compute(k):
         slot = lax.rem(k, 2)
 
         def expert(e, _):
+            pl.when(k == 0)(lambda: hidden(e).wait())
             wslot = weights_ready(5 * k + e)
-
-            def tile(j, _):
-                c = cols(j, 256)
-                o[e, :, c] = jnp.dot(hv[e], wbuf[wslot, :, c], preferred_element_type=F32).astype(BF16)
-                return 0
-
-            return lax.fori_loop(0, DK // 256, tile, 0)
+            o[e] = jnp.dot(hv[e], wbuf[wslot], preferred_element_type=F32).astype(BF16)
+            return 0
 
         lax.fori_loop(0, experts, expert, 0)
 
+        @pl.when(k == 0)
+        def _():
+            gates.wait()
+            common.wait()
+
         @pl.when(k >= 2)
         def _():
             beside(k).wait_send()
 
-        def combine(m, _):
-            rows = o[:, pl.ds(pl.multiple_of(m * 80, 80), 80), :].reshape(4 * 80, DK)
-            mine = gv[m, :, cols(at.core, 256)]
-            theirs = gv[m, :, cols(1 - at.core, 256)]
-            across = (((0,), (0,)), ((), ()))
-            acc8[m] = lax.dot_general(mine, rows, across, preferred_element_type=F32)
-            dsend[slot, m] = lax.dot_general(theirs, rows, across, preferred_element_type=F32).astype(BF16)
-            return 0
-
-        lax.fori_loop(0, 8, combine, 0)
+        def combine(m, core):
+            rows = o[:, m * 80 : (m + 1) * 80, :].reshape(4 * 80, DK)
+            return lax.dot_general(gv[m, :, cols(core, 256)], rows, (((0,), (0,)), ((), ())), preferred_element_type=F32)
+
+        for m in range(8):
+            dsend[slot, m] = combine(m, 1 - at.core).astype(BF16)
 
         @pl.when(k >= 2)
         def _():
             pl.semaphore_wait(free, 1)
 
         beside(k).start()
-
+        for m in range(8):
+            acc8[m] = combine(m, at.core)
         wslot = weights_ready(5 * k + 4)
-
-        def tile(j, _):
-            c = cols(j, 256)
-            acc8[0, :, c] += jnp.dot(hsv[...], wbuf[wslot, :, c], preferred_element_type=F32)
-            return 0
-
-        lax.fori_loop(0, DK // 256, tile, 0)
+        acc8[0] += jnp.dot(hsv[...], wbuf[wslot], preferred_element_type=F32)
 
     def send_when_free(stage, k, p):
         @pl.when(k >= 2)
@@ -513,7 +513,7 @@
             vmem((3, DK, 2 * ff), BF16),
             vmem((experts, rows, 2 * ff), F32),
             vmem((tokens, 2 * ff), F32),
-            vmem((8, 8 * slots, 2 * tokens), BF16),
+            vmem((8, 2, experts * slots, tokens), BF16),
             vmem((8 * slots, 2 * tokens), BF16),
             vmem((2, 64, ff), BF16),
             dma,
@@ -555,7 +555,7 @@
             vmem((2, tokens, DK), F32),
             *by_part(2, 4), *by_part(2, 2), *by_part(2, 1),
             *by_part(chunks, 4), *by_part(chunks, 2), *by_part(chunks, 1),
-            dma((3,)),
+            dma((6,)),
             dma((3,)),
             dma((2,)),
             dma((2,)),

time: 383 us -> 292 us (0.76)
  Pallas kernels: 377 us -> 286 us
    pallas_call x1, Pallas kernels: 233 us -> 156 us  [layer(): pl.pallas_call(gather_kernel, name='gather_up', out_shape=[shape((experts...]
    pallas_call x1, Pallas kernels: 144 us -> 130 us  [layer(): pl.pallas_call(scatter_kernel, name='down_scatter', out_shape=shape((toke...]
where the time goes in v2:
time: 292 us
  Pallas kernels  286 us (98%)
  local copies, waits for them, and re-layouts  3.13 us (1%)
    pallas_call x1, Pallas kernels, layer(): pl.pallas_call(gather_kernel, name='gather_up', out_shape=[shape((experts...  156 us
    pallas_call x1, Pallas kernels, layer(): pl.pallas_call(scatter_kernel, name='down_scatter', out_shape=shape((toke...  130 us

profile of v2, /device:TPU:0, one launch (start us, length us, event | category | flops | bytes accessed | tf_op | source)
XLA Modules:
  0.0 291.6 jit_solution(5760244202585301848)
XLA Ops:
  0.0 0.7 convert_bitcast_fusion
  0.7 1.3 maximum_bitcast_fusion.route
  2.0 156.2 %gather_up.1 = (bf16[4,640,1408]{2,1,0:T(8,128)(2,1)}, bf16[256,1408]{1,0:T(8,128)(2,1)}, bf16[8,320,512]{2,1,0:T(8,128)(2,1)}, bf16[8,8,96,512]{3,2,1,0:T(8,128...) custom-call(bf16[256,4096]{1,0:T(8,128)(2,1)} %bitcast.8, ...), custom_call_target="tpu_custom_call" | custom-call | tf_op jit(solution)/shard_map/gather_up/pallas_call | solution.py:502
  158.2 130.2 %down_scatter.1 = bf16[256,4096]{1,0:T(8,128)(2,1)} custom-call(bf16[4,640,1408]{2,1,0:T(8,128)(2,1)} %get-tuple-element.8.h, bf16[256,1408]{1,0:T(8,128)(2,1)} %get-tuple-element.9.hs, bf16[8,320,512]{2,1,0:T(8,128)(2,1)} %get-tuple-element.10.g, bf16[4,1408,4096]{2,1,0:T(8,128)(2,1)} %wd.1, bf16[1408,4096]{1,0:T(8,128)(2,1)} %sd.1), custom_call_target="tpu_custom_call" | custom-call | tf_op jit(solution)/shard_map/down_scatter/pallas_call | solution.py:538
  288.5 3.1 %copy.12 = bf16[1,1,256,4096]{3,2,1,0:T(8,128)(2,1)} copy(bf16[1,1,256,4096]{3,2,1,0:T(8,128)(2,1)} %bitcast.7) | data formatting | bytes 4194304

commit v3 on v2

v3 whole, which is shorter than its diff:
```python
import functools

import jax
import jax.numpy as jnp
from jax import lax
from jax.experimental import pallas as pl
from jax.experimental.pallas import tpu as pltpu
from jax.sharding import PartitionSpec as P

MESH = pl.DeviceIdType.MESH
DK = 512
DN = 256
PARTS = ((0, 96), (96, 80), (176, 80))
LIMIT = 67_000_000
TAIL_UP, TAIL_DOWN = 3, 1
AHEAD = 2
F32, BF16 = jnp.float32, jnp.bfloat16


class Place:
    def __init__(self):
        self.me = lax.axis_index("ep")
        self.bits = [lax.rem(lax.div(self.me, m), 2) for m in (8, 4, 2)]
        self.core = lax.rem(self.me, 2)
        self.partner = self.me + 1 - 2 * self.core

    def across(self, d):
        ids = [self.me + m * (1 - 2 * b) for m, b in zip((8, 4, 2), self.bits)]
        return ids[0] * lax.div((1 - d) * (2 - d), 2) + ids[1] * (d * (2 - d)) + ids[2] * lax.div(d * (d - 1), 2)

    def chip(self, m):
        ms = (lax.div(m, 4), lax.rem(lax.div(m, 2), 2), lax.rem(m, 2))
        x, y, z = (b + s * (1 - 2 * b) for b, s in zip(self.bits, ms))
        return ((x * 2 + y) * 2 + z) * 2


def turn(o, i):
    return lax.rem(o + i, 3)


def chip_at(o, pos):
    m = 0
    for i in range(3):
        if pos >> i & 1:
            d = turn(o, i)
            m = m + 4 - 2 * d + lax.div(d * (d - 1), 2)
    return m


def cols(k, width):
    return pl.ds(pl.multiple_of(k * width, width), width)


class Chunks:
    def __init__(self, d_model, tail):
        self.count = 1 + (d_model - (1 + tail) * DN) // DK + tail
        self.tail = self.count - tail

    def width(self, k):
        return DK if 0 < k < self.tail else DN

    def of(self, k, width):
        if isinstance(k, int):
            start = sum(self.width(i) for i in range(k))
        else:
            started = lax.div(k + self.count - 1, self.count)
            late = (k - self.tail) * lax.div(k, self.tail + 1)
            start = k * DK - (DK - DN) * (started + late)
        return pl.ds(pl.multiple_of(start, DN), width)

    def when(self, cond, k, work):
        narrow = jnp.logical_or(k == 0, jnp.logical_and(k >= self.tail, k < self.count))
        wide = jnp.logical_and(k > 0, k < self.tail)
        pl.when(jnp.logical_and(cond, narrow))(lambda: work(k, DN))
        pl.when(jnp.logical_and(cond, wide))(lambda: work(k, DK))


def gather_kernel(
    x, route, wg, wu, sg, su,
    h_out, hs_out, g_out, r0, r1, r2, q0, q1, q2,
    rt, xv, z, wbuf, acc, accs, sbuf, gbuf, hbuf,
    route_send, route_recv, fill, send, recv1, recv2, recv3, drecv, load, wsem, gsem, hsem,
):
    at = Place()
    me = at.me
    tokens, d_model = x.shape
    part = Chunks(d_model, TAIL_UP)
    chunks = part.count
    experts, slots = 4, 40
    ff = wg.shape[2]
    r, q = (r0, r1, r2), (q0, q1, q2)

    def remote(src, dst, s, v, dev):
        return pltpu.make_async_remote_copy(
            src_ref=src, dst_ref=dst, send_sem=s, recv_sem=v, device_id={"ep": dev}, device_id_type=MESH
        )

    def first(k, w, p):
        row, size = PARTS[p]
        src, dst = x.at[pl.ds(row, size), part.of(k, w)], r[p].at[k, 1, :, pl.ds(0, w)]
        return remote(src, dst, send.at[0, p], recv1.at[p, k], at.across(turn(k, p)))

    def onward(k, w, p, i):
        n = 2 << i
        src, dst = r[p].at[k, pl.ds(0, n), :, pl.ds(0, w)], r[p].at[k, pl.ds(n, n), :, pl.ds(0, w)]
        return remote(src, dst, send.at[1 + i, p], (recv2, recv3)[i].at[p, k], at.across(turn(k, p + 1 + i)))

    def beside(k, w, p, i):
        half = pl.ds(4 * i, 4)
        src, dst = r[p].at[k, half, :, pl.ds(0, w)], q[p].at[k, half, :, pl.ds(0, w)]
        return remote(src, dst, send.at[3 + i, p], drecv.at[i, p, k], at.partner)

    def filled(k, w, p):
        row, size = PARTS[p]
        return pltpu.make_async_copy(
            x.at[pl.ds(row, size), part.of(k, w)], r[p].at[k, 0, :, pl.ds(0, w)], fill.at[p, k]
        )

    def weights(i):
        slot = lax.rem(i, 3)

        def fetch(gate, up, k, w):
            rows = part.of(k, w)
            for ref, start in ((gate, 0), (up, ff)):
                dst = wbuf.at[slot, pl.ds(0, w), pl.ds(start, ff)]
                pltpu.make_async_copy(ref.at[rows], dst, wsem.at[slot]).start()

        def common(k):
            part.when(True, k, lambda k, w: fetch(sg, su, k, w))

        def routed(e, k):
            part.when(True, k, lambda k, w: fetch(wg.at[e], wu.at[e], k, w))

        rest = i - chunks
        pl.when(rest < 0)(lambda: common(i))
        pl.when(rest >= 0)(lambda: routed(lax.rem(rest, 4), lax.div(rest, 4)))

    def weights_ready(i, w):
        slot = lax.rem(i, 3)
        rows = wbuf.at[slot, pl.ds(0, w)]
        pltpu.make_async_copy(rows, rows, wsem.at[slot]).wait()
        weights(i + 2)
        return slot

    def load_rows(k, w, src, core, i):
        slot = lax.rem(k, 2)
        for p, (row, size) in enumerate(PARTS):
            o = turn(k, p)
            for pos in range(8):
                rows = pl.ds(pl.multiple_of(core * tokens + row, 16), size)
                dst = xv.at[slot, chip_at(o, pos), rows, pl.ds(0, w)]
                pltpu.make_async_copy(src[p].at[k, pos, :, pl.ds(0, w)], dst, load.at[slot, i]).start()

    def rows_ready(k, w, i):
        slot = lax.rem(k, 2)
        half = xv.at[slot, :, pl.ds(0, tokens), pl.ds(0, w)]
        pltpu.make_async_copy(half, half, load.at[slot, i]).wait()

    def begin(k, w):
        for p in range(3):
            first(k, w, p).start()

    for k in range(AHEAD):
        begin(k, part.width(k))
    weights(0)
    weights(1)
    for k in range(chunks):
        for p in range(3):
            filled(k, part.width(k), p).start()
    for j in range(1, 16):
        dev = lax.rem(me + j, 16)
        remote(route, rt.at[me], route_send, route_recv.at[me], dev).start()
    rt[me] = route[...]

    def build(m):
        base = at.chip(m)
        row = lax.broadcasted_iota(jnp.int32, (slots, tokens), 0)
        none = jnp.zeros((slots, tokens), F32)

        slot = lax.rem(m, 2)

        @pl.when(m >= 2)
        def _():
            pltpu.make_async_copy(gbuf.at[slot], g_out.at[m - 2], gsem.at[slot]).wait()

        for c in range(2):
            table = rt[base + c]
            hits = []
            for e in range(experts):
                want = (row + (me * experts + e) * slots).astype(F32)
                s, g = none, none
                for j in range(8):
                    hit = want == table[j : j + 1]
                    s = jnp.where(hit, 1.0, s)
                    g = jnp.where(hit, table[8 + j : 9 + j], g)
                hits.append(s)
                both = jnp.concatenate([g, none] if c == 0 else [none, g], axis=0)
                gbuf[slot, e * 80 : (e + 1) * 80, c * tokens : (c + 1) * tokens] = both.astype(BF16)
            sbuf[m, c] = jnp.concatenate(hits, axis=0).astype(BF16)
        pltpu.make_async_copy(gbuf.at[slot], g_out.at[m], gsem.at[slot]).start()

    def accumulate(ref, k, w, a, b):
        if w == DN:

            @pl.when(k == 0)
            def _():
                ref[...] = jnp.dot(a[...], b[...], preferred_element_type=F32)

            @pl.when(k > 0)
            def _():
                ref[...] += jnp.dot(a[...], b[...], preferred_element_type=F32)
        else:
            ref[...] += jnp.dot(a[...], b[...], preferred_element_type=F32)

    def shared(i, w):
        slot = weights_ready(i, w)
        accumulate(accs, i, w, x.at[:, part.of(i, w)], wbuf.at[slot, pl.ds(0, w)])

    def hidden(src, dst, i, rows):
        slot = lax.rem(i, 8)

        @pl.when(i >= 8)
        def _():
            pltpu.make_async_copy(hbuf.at[slot], dst, hsem.at[slot]).wait()

        a = src[rows, pl.ds(0, ff)]
        hbuf[slot] = (a * jax.nn.sigmoid(a) * src[rows, pl.ds(ff, ff)]).astype(BF16)
        pltpu.make_async_copy(hbuf.at[slot], dst, hsem.at[slot]).start()

    def hidden_shared():
        def one(i, _):
            rows = pl.ds(pl.multiple_of(i * 64, 64), 64)
            hidden(accs, hs_out.at[rows], i, rows)
            return 0

        lax.fori_loop(0, tokens // 64, one, 0)

    def hidden_routed(e):
        def one(i, _):
            rows = pl.ds(pl.multiple_of(i * 64, 64), 64)
            hidden(acc.at[e], h_out.at[e, rows], tokens // 64 + 10 * e + i, rows)
            return 0

        lax.fori_loop(0, 10, one, 0)

    def gathered(k, w):
        for p in range(3):
            onward(k, w, p, 1).wait_recv()
            beside(k, w, p, 1).start()
        load_rows(k, w, r, at.core, 0)

    def exchanged(k, w):
        for p in range(3):
            beside(k, w, p, 0).wait_recv()
            beside(k, w, p, 1).wait_recv()
        load_rows(k, w, q, 1 - at.core, 1)

    def compute(k, w):
        slot = lax.rem(k, 2)
        rows_ready(k, w, 0)
        rows_ready(k, w, 1)
        for m in range(8):
            d = [
                jnp.dot(sbuf[m, c], xv[slot, m, c * tokens : (c + 1) * tokens, :w], preferred_element_type=F32)
                for c in range(2)
            ]
            for e in range(experts):
                mine = [v[e * slots : (e + 1) * slots] for v in d]
                z[e, m * 80 : (m + 1) * 80, :w] = jnp.concatenate(mine, axis=0).astype(BF16)

        def expert(e, _):
            part.when(e == 1, k + 2, third)
            part.when(e == 2, k + 1, gathered)
            part.when(e == 3, k + 1, exchanged)
            wslot = weights_ready(chunks + 4 * k + e, w)
            accumulate(acc.at[e], k, w, z.at[e, :, pl.ds(0, w)], wbuf.at[wslot, pl.ds(0, w)])
            if w == DN:
                pl.when(k == chunks - 1)(lambda: hidden_routed(e))
            return 0

        lax.fori_loop(0, experts, expert, 0)

    def second(k, w):
        for p in range(3):
            filled(k, w, p).wait()
            first(k, w, p).wait_recv()
            onward(k, w, p, 0).start()

    def third(k, w):
        for p in range(3):
            onward(k, w, p, 0).wait_recv()
            onward(k, w, p, 1).start()
            beside(k, w, p, 0).start()

    def tables():
        for j in range(1, 16):
            b = lax.rem(me + j, 16)
            remote(route, rt.at[b], route_send, route_recv.at[b], b).wait_recv()

        def one(m, _):
            build(m)
            return 0

        lax.fori_loop(0, 8, one, 0)
        for slot in range(2):
            pltpu.make_async_copy(gbuf.at[slot], g_out.at[slot], gsem.at[slot]).wait()

    def shared_between(lo, hi):
        def one(i, _):
            part.when(True, i, shared)
            return 0

        lax.fori_loop(lo, hi, one, 0)

    def step(s, _):
        pl.when(s == 0)(lambda: shared_between(0, 3))
        part.when(s == 2, s - 1, third)
        part.when(True, s, second)
        part.when(True, s + AHEAD, begin)
        pl.when(s == 1)(lambda: shared_between(3, 6))
        part.when(s == 1, s - 1, third)
        pl.when(s == 1)(tables)
        pl.when(s == 2)(lambda: shared_between(6, chunks))
        part.when(s == 2, s - 2, gathered)
        part.when(s == 2, s - 2, exchanged)
        part.when(True, s - 3, compute)
        pl.when(s == 3)(hidden_shared)
        return 0

    lax.fori_loop(0, chunks + 3, step, 0)

    for slot in range(8):
        pltpu.make_async_copy(hbuf.at[slot], hs_out.at[pl.ds(0, 64)], hsem.at[slot]).wait()

    remote(rt.at[pl.ds(0, 15)], rt.at[pl.ds(0, 15)], route_send, route_recv.at[0], at.partner).wait_send()
    for p in range(3):
        for i, rows in enumerate((pl.ds(0, 1), pl.ds(0, 2), pl.ds(0, 4), pl.ds(0, 4), pl.ds(4, 4))):
            sent = r[p].at[pl.ds(0, d_model // DK), rows]
            remote(sent, sent, send.at[i, p], recv1.at[p, 0], at.partner).wait_send()


def scatter_kernel(
    h, hs, g, wd, sd,
    y,
    hv, hsv, gv, wbuf, o, dsend, dland, acc8, acc4, acc2, acc1,
    as0, as1, as2, bs0, bs1, bs2, cs0, cs1, cs2,
    al0, al1, al2, bl0, bl1, bl2, cl0, cl1, cl2,
    start_sem, wsem, dsend_sem, drecv, free, asend_sem, bsend_sem, csend_sem, arecv, brecv, crecv,
):
    at = Place()
    tokens, d_model = y.shape
    part = Chunks(d_model, TAIL_DOWN)
    chunks = part.count
    experts = h.shape[0]
    ff = h.shape[2]
    a_send, b_send, c_send = (as0, as1, as2), (bs0, bs1, bs2), (cs0, cs1, cs2)
    a_land, b_land, c_land = (al0, al1, al2), (bl0, bl1, bl2), (cl0, cl1, cl2)

    def remote(src, dst, s, v, dev):
        return pltpu.make_async_remote_copy(
            src_ref=src, dst_ref=dst, send_sem=s, recv_sem=v, device_id={"ep": dev}, device_id_type=MESH
        )

    def beside(k, w):
        slot = lax.rem(k, 2)
        src, dst = dsend.at[slot, :, :, pl.ds(0, w)], dland.at[slot, :, :, pl.ds(0, w)]
        return remote(src, dst, dsend_sem.at[slot], drecv.at[slot], at.partner)

    def hop(stage, k, w, p):
        slot = lax.rem(k, 2)
        src, dst = (a_send, b_send, c_send)[stage][p], (a_land, b_land, c_land)[stage][p]
        sems, lands = (asend_sem, bsend_sem, csend_sem)[stage], (arecv, brecv, crecv)[stage]
        src, dst = src.at[slot, :, :, pl.ds(0, w)], dst.at[k, :, :, pl.ds(0, w)]
        return remote(src, dst, sems.at[p, slot], lands.at[p, k], at.across(turn(k, p + 2 - stage)))

    def weights(i):
        slot = lax.rem(i, 3)
        e = lax.rem(i, 5)

        def fetch(k, w):
            dst = wbuf.at[slot, :, pl.ds(0, w)]
            pl.when(e < 4)(lambda: pltpu.make_async_copy(wd.at[e, :, part.of(k, w)], dst, wsem.at[slot]).start())
            pl.when(e == 4)(lambda: pltpu.make_async_copy(sd.at[:, part.of(k, w)], dst, wsem.at[slot]).start())

        part.when(True, lax.div(i, 5), fetch)

    def weights_ready(i, w):
        slot = lax.rem(i, 3)
        columns = wbuf.at[slot, :, pl.ds(0, w)]
        pltpu.make_async_copy(columns, columns, wsem.at[slot]).wait()
        weights(i + 2)
        return slot

    def hidden(e):
        return pltpu.make_async_copy(h.at[e], hv.at[e], start_sem.at[e])

    common = pltpu.make_async_copy(hs, hsv, start_sem.at[4])
    gates = pltpu.make_async_copy(g, gv, start_sem.at[5])
    hidden(0).start()
    weights(0)
    hidden(1).start()
    weights(1)
    for copy in (hidden(2), hidden(3), gates, common):
        copy.start()

    def compute(k, w):
        slot = lax.rem(k, 2)

        def expert(e, _):
            pl.when(k == 0)(lambda: hidden(e).wait())
            wslot = weights_ready(5 * k + e, w)
            o[e, :, :w] = jnp.dot(hv[e], wbuf[wslot, :, :w], preferred_element_type=F32).astype(BF16)
            return 0

        lax.fori_loop(0, experts, expert, 0)

        @pl.when(k == 0)
        def _():
            gates.wait()
            common.wait()

        sent(k, lambda v: beside(k, v).wait_send())

        def combine(m, core):
            rows = o[:, m * 80 : (m + 1) * 80, :w].reshape(4 * 80, w)
            return lax.dot_general(gv[m, :, cols(core, 256)], rows, (((0,), (0,)), ((), ())), preferred_element_type=F32)

        for m in range(8):
            dsend[slot, m, :, :w] = combine(m, 1 - at.core).astype(BF16)

        @pl.when(k >= 2)
        def _():
            pl.semaphore_wait(free, 1)

        beside(k, w).start()
        for m in range(8):
            acc8[m, :, :w] = combine(m, at.core)
        wslot = weights_ready(5 * k + 4, w)
        acc8[0, :, :w] += jnp.dot(hsv[...], wbuf[wslot, :, :w], preferred_element_type=F32)

    def sent(k, wait):
        narrow = jnp.logical_or(k == 2, k - 2 >= part.tail)
        pl.when(narrow)(lambda: wait(DN))
        pl.when(jnp.logical_and(k > 2, k - 2 < part.tail))(lambda: wait(DK))

    def first(k, w):
        slot = lax.rem(k, 2)
        beside(k, w).wait_recv()
        for p, (row, size) in enumerate(PARTS):
            sent(k, lambda v: hop(0, k, v, p).wait_send())
            for pos in range(7, -1, -1):
                m = chip_at(turn(k, p), pos)
                v = acc8[m, row : row + size, :w] + dland[slot, m, row : row + size, :w].astype(F32)
                if pos >= 4:
                    a_send[p][slot, pos - 4, :, :w] = v.astype(BF16)
                else:
                    acc4[slot, pos, row : row + size, :w] = v
                if pos == 4:
                    hop(0, k, w, p).start()

        @pl.when(k + 2 < chunks)
        def _():
            pl.semaphore_signal(free, inc=1, device_id={"ep": at.partner}, device_id_type=MESH)

    def second(k, w):
        slot = lax.rem(k, 2)
        for p, (row, size) in enumerate(PARTS):
            hop(0, k, w, p).wait_recv()
            sent(k, lambda v: hop(1, k, v, p).wait_send())
            for pos in range(3, -1, -1):
                v = acc4[slot, pos, row : row + size, :w] + a_land[p][k, pos, :, :w].astype(F32)
                if pos >= 2:
                    b_send[p][slot, pos - 2, :, :w] = v.astype(BF16)
                else:
                    acc2[slot, pos, row : row + size, :w] = v
                if pos == 2:
                    hop(1, k, w, p).start()

    def third(k, w):
        slot = lax.rem(k, 2)
        for p, (row, size) in enumerate(PARTS):
            hop(1, k, w, p).wait_recv()
            sent(k, lambda v: hop(2, k, v, p).wait_send())
            for pos in (1, 0):
                v = acc2[slot, pos, row : row + size, :w] + b_land[p][k, pos, :, :w].astype(F32)
                if pos == 1:
                    c_send[p][slot, 0, :, :w] = v.astype(BF16)
                    hop(2, k, w, p).start()
                else:
                    acc1[slot, row : row + size, :w] = v

    def last(k, w):
        slot = lax.rem(k, 2)
        for p, (row, size) in enumerate(PARTS):
            hop(2, k, w, p).wait_recv()
            out = acc1[slot, row : row + size, :w] + c_land[p][k, 0, :, :w].astype(F32)
            y[row : row + size, part.of(k, w)] = out.astype(BF16)

    def step(s, _):
        for stage, work in ((1, first), (0, compute), (2, second), (3, third), (4, last)):
            part.when(True, s - stage, work)
        return 0

    lax.fori_loop(0, chunks + 4, step, 0)
    for k, w in ((chunks - 2, part.width(chunks - 2)), (chunks - 1, DN)):
        beside(k, w).wait_send()
        for stage in range(3):
            for p in range(3):
                hop(stage, k, w, p).wait_send()


def layer(x, expert, slot, gate, w_gate, w_up, w_down, s_gate, s_up, s_down):
    tokens, d_model = x.shape[2:]
    top = expert.shape[3]
    experts, _, ff = w_gate.shape
    slots = 5 * tokens * top // (4 * 64)
    chunks, chunks_down = Chunks(d_model, TAIL_UP).count, Chunks(d_model, TAIL_DOWN).count
    rows = 16 * slots
    x = x.reshape(tokens, d_model)
    kept = jnp.where(slot < slots, expert * slots + slot, -1).astype(F32)
    route = jnp.concatenate([kept.reshape(tokens, top), gate.reshape(tokens, top)], axis=1).T

    dma, vmem, anyw = pltpu.SemaphoreType.DMA, pltpu.VMEM, pl.BlockSpec(memory_space=pl.ANY)
    here = pl.BlockSpec(memory_space=pltpu.VMEM)
    shape = jax.ShapeDtypeStruct
    landing = [shape((chunks, 8, size, DK), BF16) for _, size in PARTS]
    h, hs, g, *_ = pl.pallas_call(
        gather_kernel,
        name="gather_up",
        out_shape=[shape((experts, rows, ff), BF16), shape((tokens, ff), BF16), shape((8, 8 * slots, 2 * tokens), BF16)]
        + landing * 2,
        in_specs=[here, here] + [anyw] * 4,
        out_specs=[anyw] * 9,
        scratch_shapes=[
            vmem((16, 2 * top, tokens), F32),
            vmem((2, 8, 2 * tokens, DK), BF16),
            vmem((experts, rows, DK), BF16),
            vmem((3, DK, 2 * ff), BF16),
            vmem((experts, rows, 2 * ff), F32),
            vmem((tokens, 2 * ff), F32),
            vmem((8, 2, experts * slots, tokens), BF16),
            vmem((2, 8 * slots, 2 * tokens), BF16),
            vmem((8, 64, ff), BF16),
            dma,
            dma((16,)),
            dma((3, chunks)),
            dma((5, 3)),
            dma((3, chunks)),
            dma((3, chunks)),
            dma((3, chunks)),
            dma((2, 3, chunks)),
            dma((2, 2)),
            dma((3,)),
            dma((2,)),
            dma((8,)),
        ],
        compiler_params=pltpu.CompilerParams(has_side_effects=True, vmem_limit_bytes=LIMIT),
    )(x, route, w_gate, w_up, s_gate, s_up)

    def by_part(lead, count):
        return [vmem((lead, count, size, DK), BF16) for _, size in PARTS]

    y = pl.pallas_call(
        scatter_kernel,
        name="down_scatter",
        out_shape=shape((tokens, d_model), BF16),
        in_specs=[anyw] * 5,
        out_specs=here,
        scratch_shapes=[
            vmem((experts, rows, ff), BF16),
            vmem((tokens, ff), BF16),
            vmem((8, 8 * slots, 2 * tokens), BF16),
            vmem((3, ff, DK), BF16),
            vmem((experts, rows, DK), BF16),
            vmem((2, 8, tokens, DK), BF16),
            vmem((2, 8, tokens, DK), BF16),
            vmem((8, tokens, DK), F32),
            vmem((2, 4, tokens, DK), F32),
            vmem((2, 2, tokens, DK), F32),
            vmem((2, tokens, DK), F32),
            *by_part(2, 4), *by_part(2, 2), *by_part(2, 1),
            *by_part(chunks_down, 4), *by_part(chunks_down, 2), *by_part(chunks_down, 1),
            dma((6,)),
            dma((3,)),
            dma((2,)),
            dma((2,)),
            pltpu.SemaphoreType.REGULAR,
            dma((3, 2)),
            dma((3, 2)),
            dma((3, 2)),
            dma((3, chunks_down)),
            dma((3, chunks_down)),
            dma((3, chunks_down)),
        ],
        compiler_params=pltpu.CompilerParams(has_side_effects=True, vmem_limit_bytes=LIMIT),
    )(h, hs, g, w_down, s_down)
    return y.reshape(1, 1, tokens, d_model)


def solution(mesh):
    by_device, by_expert = P("dp", "ep", None, None), P("ep", None, None)
    return jax.shard_map(
        layer,
        mesh=mesh,
        in_specs=(by_device,) * 4 + (by_expert,) * 3 + (P(None, None),) * 3,
        out_specs=by_device,
        check_vma=False,
    )
```

time: 292 us -> 280 us (0.959)
  Pallas kernels: 286 us -> 275 us
    pallas_call x1, Pallas kernels: 156 us -> 142 us  [layer(): pl.pallas_call(gather_kernel, name='gather_up', out_shape=[shape((experts...]
where the time goes in v3:
time: 280 us
  Pallas kernels  275 us (98%)
  local copies, waits for them, and re-layouts  3.13 us (1%)
    pallas_call x1, Pallas kernels, layer(): pl.pallas_call(gather_kernel, name='gather_up', out_shape=[shape((experts...  142 us
    pallas_call x1, Pallas kernels, layer(): pl.pallas_call(scatter_kernel, name='down_scatter', out_shape=shape((toke...  133 us

profile of v3, /device:TPU:0, one launch (start us, length us, event | category | flops | bytes accessed | tf_op | source)
XLA Modules:
  0.0 279.8 jit_solution(4868215011698902735)
XLA Ops:
  0.0 0.7 convert_bitcast_fusion
  0.7 1.3 maximum_bitcast_fusion.route
  2.0 141.6 %gather_up.1 = (bf16[4,640,1408]{2,1,0:T(8,128)(2,1)}, bf16[256,1408]{1,0:T(8,128)(2,1)}, bf16[8,320,512]{2,1,0:T(8,128)(2,1)}, bf16[10,8,96,512]{3,2,1,0:T(8,12...) custom-call(bf16[256,4096]{1,0:T(8,128)(2,1)} %bitcast.8, ...), custom_call_target="tpu_custom_call" | custom-call | tf_op jit(solution)/shard_map/gather_up/pallas_call | solution.py:527
  143.6 133.0 %down_scatter.1 = bf16[256,4096]{1,0:T(8,128)(2,1)} custom-call(bf16[4,640,1408]{2,1,0:T(8,128)(2,1)} %get-tuple-element.8.h, bf16[256,1408]{1,0:T(8,128)(2,1)} %get-tuple-element.9.hs, bf16[8,320,512]{2,1,0:T(8,128)(2,1)} %get-tuple-element.10.g, bf16[4,1408,4096]{2,1,0:T(8,128)(2,1)} %wd.1, bf16[1408,4096]{1,0:T(8,128)(2,1)} %sd.1), custom_call_target="tpu_custom_call" | custom-call | tf_op jit(solution)/shard_map/down_scatter/pallas_call | solution.py:563
  276.6 3.1 %copy.12 = bf16[1,1,256,4096]{3,2,1,0:T(8,128)(2,1)} copy(bf16[1,1,256,4096]{3,2,1,0:T(8,128)(2,1)} %bitcast.7) | data formatting | bytes 4194304

commit v4 on v3

--- a/solution.py
+++ b/solution.py
@@ -12,7 +12,8 @@
 DN = 256
 PARTS = ((0, 96), (96, 80), (176, 80))
 LIMIT = 67_000_000
-TAIL_UP, TAIL_DOWN = 3, 1
+TAIL_UP, TAIL_DOWN = 1, 1
+SHARED_FIRST = 1
 AHEAD = 2
 F32, BF16 = jnp.float32, jnp.bfloat16
 
@@ -159,18 +160,6 @@
     def begin(k, w):
         for p in range(3):
             first(k, w, p).start()
-
-    for k in range(AHEAD):
-        begin(k, part.width(k))
-    weights(0)
-    weights(1)
-    for k in range(chunks):
-        for p in range(3):
-            filled(k, part.width(k), p).start()
-    for j in range(1, 16):
-        dev = lax.rem(me + j, 16)
-        remote(route, rt.at[me], route_send, route_recv.at[me], dev).start()
-    rt[me] = route[...]
 
     def build(m):
         base = at.chip(m)
@@ -313,7 +302,7 @@
         lax.fori_loop(lo, hi, one, 0)
 
     def step(s, _):
-        pl.when(s == 0)(lambda: shared_between(0, 3))
+        pl.when(s == 0)(lambda: shared_between(SHARED_FIRST, 3))
         part.when(s == 2, s - 1, third)
         part.when(True, s, second)
         part.when(True, s + AHEAD, begin)
@@ -326,6 +315,23 @@
         part.when(True, s - 3, compute)
         pl.when(s == 3)(hidden_shared)
         return 0
+
+    entry = pltpu.get_barrier_semaphore()
+    for j in range(1, 16):
+        pl.semaphore_signal(entry, inc=1, device_id={"ep": lax.rem(me + j, 16)}, device_id_type=MESH)
+    weights(0)
+    weights(1)
+    for k in range(chunks):
+        for p in range(3):
+            filled(k, part.width(k), p).start()
+    rt[me] = route[...]
+    shared_between(0, SHARED_FIRST)
+    pl.semaphore_wait(entry, 15)
+    for k in range(AHEAD):
+        begin(k, part.width(k))
+    for j in range(1, 16):
+        dev = lax.rem(me + j, 16)
+        remote(route, rt.at[me], route_send, route_recv.at[me], dev).start()
 
     lax.fori_loop(0, chunks + 3, step, 0)
 
@@ -391,6 +397,10 @@
         weights(i + 2)
         return slot
 
+    entry = pltpu.get_barrier_semaphore()
+    for peer in (at.partner, *(at.across(d) for d in range(3))):
+        pl.semaphore_signal(entry, inc=1, device_id={"ep": peer}, device_id_type=MESH)
+
     def hidden(e):
         return pltpu.make_async_copy(h.at[e], hv.at[e], start_sem.at[e])
 
@@ -400,8 +410,7 @@
     weights(0)
     hidden(1).start()
     weights(1)
-    for copy in (hidden(2), hidden(3), gates, common):
-        copy.start()
+    pl.semaphore_wait(entry, 4)
 
     def compute(k, w):
         slot = lax.rem(k, 2)
@@ -409,6 +418,12 @@
         def expert(e, _):
             pl.when(k == 0)(lambda: hidden(e).wait())
             wslot = weights_ready(5 * k + e, w)
+
+            @pl.when(jnp.logical_and(k == 0, e == 0))
+            def _():
+                for copy in (hidden(2), hidden(3), gates, common):
+                    copy.start()
+
             o[e, :, :w] = jnp.dot(hv[e], wbuf[wslot, :, :w], preferred_element_type=F32).astype(BF16)
             return 0
 
@@ -554,7 +569,7 @@
             dma((2,)),
             dma((8,)),
         ],
-        compiler_params=pltpu.CompilerParams(has_side_effects=True, vmem_limit_bytes=LIMIT),
+        compiler_params=pltpu.CompilerParams(collective_id=1, has_side_effects=True, vmem_limit_bytes=LIMIT),
     )(x, route, w_gate, w_up, s_gate, s_up)
 
     def by_part(lead, count):
@@ -592,7 +607,7 @@
             dma((3, chunks_down)),
             dma((3, chunks_down)),
         ],
-        compiler_params=pltpu.CompilerParams(has_side_effects=True, vmem_limit_bytes=LIMIT),
+        compiler_params=pltpu.CompilerParams(collective_id=0, has_side_effects=True, vmem_limit_bytes=LIMIT),
     )(h, hs, g, w_down, s_down)
     return y.reshape(1, 1, tokens, d_model)
 

time: 280 us -> 275 us (0.982)
  Pallas kernels: 275 us -> 270 us
    pallas_call x1, Pallas kernels: 133 us -> 129 us  [layer(): pl.pallas_call(scatter_kernel, name='down_scatter', out_shape=shape((toke...]
where the time goes in v4:
time: 275 us
  Pallas kernels  270 us (98%)
  local copies, waits for them, and re-layouts  3.13 us (1%)
    pallas_call x1, Pallas kernels, layer(): pl.pallas_call(gather_kernel, name='gather_up', out_shape=[shape((experts...  140 us
    pallas_call x1, Pallas kernels, layer(): pl.pallas_call(scatter_kernel, name='down_scatter', out_shape=shape((toke...  129 us

profile of v4, /device:TPU:0, one launch (start us, length us, event | category | flops | bytes accessed | tf_op | source)
XLA Modules:
  0.0 274.8 jit_solution(8889518861040984784)
XLA Ops:
  0.0 0.7 convert_bitcast_fusion
  0.7 1.3 maximum_bitcast_fusion.route
  2.0 140.2 %gather_up.1 = (bf16[4,640,1408]{2,1,0:T(8,128)(2,1)}, bf16[256,1408]{1,0:T(8,128)(2,1)}, bf16[8,320,512]{2,1,0:T(8,128)(2,1)}, bf16[9,8,96,512]{3,2,1,0:T(8,128...) custom-call(bf16[256,4096]{1,0:T(8,128)(2,1)} %bitcast.8, ...), custom_call_target="tpu_custom_call" | custom-call | tf_op jit(solution)/shard_map/gather_up/pallas_call | solution.py:542
  142.3 129.4 %down_scatter.1 = bf16[256,4096]{1,0:T(8,128)(2,1)} custom-call(bf16[4,640,1408]{2,1,0:T(8,128)(2,1)} %get-tuple-element.8.h, bf16[256,1408]{1,0:T(8,128)(2,1)} %get-tuple-element.9.hs, bf16[8,320,512]{2,1,0:T(8,128)(2,1)} %get-tuple-element.10.g, bf16[4,1408,4096]{2,1,0:T(8,128)(2,1)} %wd.1, bf16[1408,4096]{1,0:T(8,128)(2,1)} %sd.1), custom_call_target="tpu_custom_call" | custom-call | tf_op jit(solution)/shard_map/down_scatter/pallas_call | solution.py:578
  271.7 3.1 %copy.12 = bf16[1,1,256,4096]{3,2,1,0:T(8,128)(2,1)} copy(bf16[1,1,256,4096]{3,2,1,0:T(8,128)(2,1)} %bitcast.7) | data formatting | bytes 4194304

commit v5 on v4

--- a/solution.py
+++ b/solution.py
@@ -301,10 +301,16 @@
 
         lax.fori_loop(lo, hi, one, 0)
 
+    def send_route():
+        for j in range(1, 16):
+            dev = lax.rem(me + j, 16)
+            remote(route, rt.at[me], route_send, route_recv.at[me], dev).start()
+
     def step(s, _):
         pl.when(s == 0)(lambda: shared_between(SHARED_FIRST, 3))
         part.when(s == 2, s - 1, third)
         part.when(True, s, second)
+        pl.when(s == 0)(send_route)
         part.when(True, s + AHEAD, begin)
         pl.when(s == 1)(lambda: shared_between(3, 6))
         part.when(s == 1, s - 1, third)
@@ -329,9 +335,6 @@
     pl.semaphore_wait(entry, 15)
     for k in range(AHEAD):
         begin(k, part.width(k))
-    for j in range(1, 16):
-        dev = lax.rem(me + j, 16)
-        remote(route, rt.at[me], route_send, route_recv.at[me], dev).start()
 
     lax.fori_loop(0, chunks + 3, step, 0)
 

time: 275 us -> 276 us (level)
  no operation moved by 1% of the time
where the time goes in v5:
time: 276 us; the launch traced here: 275 us
  Pallas kernels  270 us (98%)
  local copies, waits for them, and re-layouts  3.13 us (1%)
    pallas_call x1, Pallas kernels, layer(): pl.pallas_call(gather_kernel, name='gather_up', out_shape=[shape((experts...  140 us
    pallas_call x1, Pallas kernels, layer(): pl.pallas_call(scatter_kernel, name='down_scatter', out_shape=shape((toke...  130 us

profile of v5, /device:TPU:0, one launch (start us, length us, event | category | flops | bytes accessed | tf_op | source)
XLA Modules:
  0.0 275.2 jit_solution(16742530971366918531)
XLA Ops:
  0.0 0.7 convert_bitcast_fusion
  0.7 1.3 maximum_bitcast_fusion.route
  2.0 140.3 %gather_up.1 = (bf16[4,640,1408]{2,1,0:T(8,128)(2,1)}, bf16[256,1408]{1,0:T(8,128)(2,1)}, bf16[8,320,512]{2,1,0:T(8,128)(2,1)}, bf16[9,8,96,512]{3,2,1,0:T(8,128...) custom-call(bf16[256,4096]{1,0:T(8,128)(2,1)} %bitcast.8, ...), custom_call_target="tpu_custom_call" | custom-call | tf_op jit(solution)/shard_map/gather_up/pallas_call | solution.py:545
  142.3 129.7 %down_scatter.1 = bf16[256,4096]{1,0:T(8,128)(2,1)} custom-call(bf16[4,640,1408]{2,1,0:T(8,128)(2,1)} %get-tuple-element.8.h, bf16[256,1408]{1,0:T(8,128)(2,1)} %get-tuple-element.9.hs, bf16[8,320,512]{2,1,0:T(8,128)(2,1)} %get-tuple-element.10.g, bf16[4,1408,4096]{2,1,0:T(8,128)(2,1)} %wd.1, bf16[1408,4096]{1,0:T(8,128)(2,1)} %sd.1), custom_call_target="tpu_custom_call" | custom-call | tf_op jit(solution)/shard_map/down_scatter/pallas_call | solution.py:581
  272.0 3.1 %copy.12 = bf16[1,1,256,4096]{3,2,1,0:T(8,128)(2,1)} copy(bf16[1,1,256,4096]{3,2,1,0:T(8,128)(2,1)} %bitcast.7) | data formatting | bytes 4194304
